TPU v7x, 128 devices: a whole 4x4x4 slice. The times are simulated.
128 devices in a mesh: gx: 4 (over y), gy: 4 (over x), gz: 8 (over z, core).
Axes of the slice: x: 4, y: 4, z: 4, core: 2. Of those that a mesh axis runs over, the one named last changes fastest.
Arguments:
- queries: bfloat16 [65536, 1024], P(('gx', 'gy', 'gz')), may hold values from -6 to 6
- keys: bfloat16 [65536, 1024], P(('gx', 'gy', 'gz')), may hold values from -6 to 6
- values: bfloat16 [65536, 1024], P(('gx', 'gy', 'gz')), may hold values from -6 to 6
- out_grad: bfloat16 [65536, 1024], P(('gx', 'gy', 'gz')), may hold values from -0.0234375 to 0.0234375
- log_decay: float32 [4, 65536], P(None, ('gx', 'gy', 'gz')), may hold values from -0.8 to 0, as said below
- saved_states: bfloat16 [128, 4, 256, 256], P(('gx', 'gy', 'gz')), may hold values from -67.5 to 67.5
Outputs:
- query_grad: bfloat16 [65536, 1024], P(('gx', 'gy', 'gz'))
- key_grad: bfloat16 [65536, 1024], P(('gx', 'gy', 'gz'))
- value_grad: bfloat16 [65536, 1024], P(('gx', 'gy', 'gz'))
Inputs may be any that keep to these rules, and one draw needn't show every extreme that they name: `log_decay`: every entry is negative.
All inputs are finite; a program needn't handle non-finite values.
Results may differ from a plain program's by a relative error of at most 0.0056.
Values sent between devices are 32-bit elements; how exact they have to be, the bound alone decides.
A program may use at most 512 MiB of HBM per device.

v0:
```python
import jax
import jax.numpy as jnp
from jax import lax
from jax.sharding import Mesh
from jax.sharding import PartitionSpec as P

GX_GY_GZ = ("gx", "gy", "gz_0", "gz_1")


def neutral_like(value, identity):
    return jax.tree.map(
        lambda part, zero: jnp.zeros_like(part) + jnp.asarray(zero, part.dtype), value, identity
    )


def carried_in(value, axes, combine, identity):
    before = start = neutral_like(value, identity)
    subtotal = value
    for axis in reversed(axes):
        devices, index = (lax.axis_size(axis), lax.axis_index(axis))
        pieces = jax.tree.map(lambda part: lax.all_gather(part, axis), subtotal)
        inside, subtotal = (start, start)
        for k in reversed(range(devices)):
            passed = k > index
            subtotal = combine(subtotal, jax.tree.map(lambda part: part[k], pieces))
            inside = jax.tree.map(lambda new, old: jnp.where(passed, new, old), subtotal, inside)
        before = combine(inside, before)
    return before


def combine_states(earlier_part, later_part):
    return (
        earlier_part[0] * later_part[0],
        later_part[0][:, None, None] * earlier_part[1] + later_part[1],
    )


def suffix_states(element, identity):
    return carried_in(element, GX_GY_GZ, combine_states, identity)


def body(queries, keys, values, out_grad, log_decay, saved_states):
    num_heads = log_decay.shape[0]
    count_rows = queries.shape[0]
    head_width = queries.shape[1] // num_heads
    score_scale = head_width ** (-0.5)
    query_heads = queries.reshape(count_rows, num_heads, head_width)
    key_heads = keys.reshape(count_rows, num_heads, head_width)
    value_heads = values.reshape(count_rows, num_heads, head_width)
    grad_heads = out_grad.reshape(count_rows, num_heads, head_width)
    state_in = saved_states[0]
    cumulative = jnp.cumsum(log_decay, axis=1)
    block_end = cumulative[:, -1:]
    to_end = jnp.exp(block_end - cumulative)
    from_start = jnp.exp(cumulative)
    to_end_rows = to_end.T[:, :, None]
    start_rows = (score_scale * from_start).T[:, :, None]
    query_decayed = (query_heads.astype(jnp.float32) * start_rows).astype(jnp.bfloat16)
    local_grad = jnp.einsum(
        "thi,thj->hij", query_decayed, grad_heads, preferred_element_type=jnp.float32
    )
    block_decay = jnp.exp(block_end[:, 0])
    identity = (
        jnp.ones((num_heads,), jnp.float32),
        jnp.zeros((num_heads, head_width, head_width), jnp.float32),
    )
    later_grads = suffix_states((block_decay, local_grad), identity)
    grad_in = later_grads[1].astype(jnp.bfloat16)
    positions = jnp.arange(count_rows, dtype=jnp.int32)
    causal = positions[:, None] >= positions[None, :]
    log_gaps = cumulative[:, :, None] - cumulative[:, None, :]
    weight = jnp.where(causal[None], jnp.exp(jnp.minimum(log_gaps, 0.0)), 0.0)
    probs = (
        jnp.einsum("thd,shd->hts", query_heads, key_heads, preferred_element_type=jnp.float32)
        * score_scale
        * weight
    ).astype(jnp.bfloat16)
    grad_scores = (
        jnp.einsum("thd,shd->hts", grad_heads, value_heads, preferred_element_type=jnp.float32)
        * score_scale
        * weight
    ).astype(jnp.bfloat16)
    query_grad = jnp.einsum(
        "hts,shd->thd", grad_scores, key_heads, preferred_element_type=jnp.float32
    )
    query_grad = (
        query_grad
        + jnp.einsum("thj,hij->thi", grad_heads, state_in, preferred_element_type=jnp.float32)
        * start_rows
    )
    key_grad = jnp.einsum(
        "hts,thd->shd", grad_scores, query_heads, preferred_element_type=jnp.float32
    )
    key_grad = (
        key_grad
        + jnp.einsum("thj,hij->thi", value_heads, grad_in, preferred_element_type=jnp.float32)
        * to_end_rows
    )
    value_grad = jnp.einsum("hts,thd->shd", probs, grad_heads, preferred_element_type=jnp.float32)
    value_grad = (
        value_grad
        + jnp.einsum("thi,hij->thj", key_heads, grad_in, preferred_element_type=jnp.float32)
        * to_end_rows
    )
    total_width = num_heads * head_width
    return (
        query_grad.reshape(count_rows, total_width).astype(jnp.bfloat16),
        key_grad.reshape(count_rows, total_width).astype(jnp.bfloat16),
        value_grad.reshape(count_rows, total_width).astype(jnp.bfloat16),
    )


def solution(mesh):
    split = Mesh(
        mesh.devices.reshape(mesh.shape["gx"], mesh.shape["gy"], 4, 2), ("gx", "gy", "gz_0", "gz_1")
    )
    placed = (
        P(GX_GY_GZ, None),
        P(GX_GY_GZ, None),
        P(GX_GY_GZ, None),
        P(GX_GY_GZ, None),
        P(None, GX_GY_GZ),
        P(GX_GY_GZ, None, None, None),
    )
    return jax.shard_map(
        body,
        mesh=split,
        in_specs=placed,
        out_specs=(P(GX_GY_GZ, None), P(GX_GY_GZ, None), P(GX_GY_GZ, None)),
        check_vma=False,
    )
```

profile of v0, /device:TPU:1, one launch (start us, length us, event | category | flops | bytes accessed | tf_op | source)
XLA Modules:
  0.0 209.6 jit_solution(6724024158056274787)
XLA Ops:
  7.2 0.8 reshape.199
  8.0 1.2 reduce-window.6
  9.4 0.2 reduce-window.9
  9.9 1.5 copy.56
  11.4 1.5 copy.41
  12.9 1.4 fusion.7
  14.4 0.6 dynamic-slice
  15.8 3.5 %all-reduce = f32[8]{0:T(128)S(1)} all-reduce(f32[8]{0:T(128)S(1)} %bitcast_dynamic-update-slice_fusion), channel_id=2, replica_groups=mesh['gx'=4,'gy'=4,'gz_0'=4,'gz_1'=2] {'gz_1'}, use_global_device_ids=true, to_apply=%add | all-reduce | flops 8 | bytes 64
  19.3 0.6 dynamic-slice.1
  20.5 0.2 fusion.43
  20.7 10.7 %all-gather.16.cloned.1.call-done = f32[8,256,256]{2,1,0:T(8,128)} async-done(((f32[4,256,256]{2,1,0:T(8,128)}), f32[8,256,256]{2,1,0:T(8,128)}) %all-gather.16.cloned.1.call-update) | async-done | bytes 2097168 | tf_op jit(solution)/shard_map/all_gather | solution.py:21
  31.4 2.7 %bitcast_add_fusion.8 = f32[1,4,256,256]{3,2,1,0:T(8,128)} fusion(f32[8,256,256]{2,1,0:T(8,128)} %all-gather.16.cloned.1.call-done, f32[4]{0:T(128)S(1)} %get-tuple-element.31, f32[4]{0:T(128)S(1)} %get-tuple-element.32), kind=kLoop, calls=%fused_computation.47 | loop fusion | flops 786432 | bytes 3145760 | tf_op jit(solution)/shard_map/add | solution.py:34
  34.2 8.8 %all-reduce.1 = f32[16]{0:T(128)S(1)} all-reduce(f32[16]{0:T(128)S(1)} %get-tuple-element.30), channel_id=4, replica_groups=mesh['gx'=4,'gy'=4,'gz_0'=4,'gz_1'=2] {'gz_0'}, use_global_device_ids=true, to_apply=%add.1 | all-reduce | flops 16 | bytes 128
  43.1 40.4 %all-gather.10.cloned.1.call-done = f32[4,4,256,256]{3,2,1,0:T(8,128)} async-done(((f32[1,4,256,256]{3,2,1,0:T(8,128)}), f32[4,4,256,256]{3,2,1,0:T(8,128)}) %all-gather.10.cloned.1.call-update) | async-done | bytes 4194320 | tf_op jit(solution)/shard_map/all_gather | solution.py:21
  83.5 3.5 %multiply_add_fusion.1 = f32[1,4,256,256]{3,2,1,0:T(8,128)} fusion(f32[4,4,256,256]{3,2,1,0:T(8,128)} %all-gather.10.cloned.1.call-done, f32[4]{0:T(128)S(1)} %get-tuple-element.26, f32[4]{0:T(128)S(1)} %get-tuple-element.28, f32[4]{0:T(128)S(1)} %get-tuple-element.27, f32[4]{0:T(128)S(1)} %get-tuple-element.29), kind=kLoop, calls=%fused_computation.51 | loop fusion | flops 1835008 | bytes 5242944 | tf_op jit(solution)/shard_map/add | solution.py:34
  87.1 7.6 %all-gather.3 = f32[4,1,4]{2,1,0:T(1,128)S(1)} all-gather(f32[1,1,4]{2,1,0:T(1,128)S(1)} %get-tuple-element.25), channel_id=1, replica_groups=mesh['gx'=4,'gy'=4,'gz_0'=4,'gz_1'=2] {'gy'}, dimensions={0}, use_global_device_ids=true | all-gather | bytes 80 | tf_op jit(solution)/shard_map/all_gather | solution.py:21
  94.7 40.8 %all-gather.12.cloned.1.call-done = f32[4,4,256,256]{3,2,1,0:T(8,128)} async-done(((f32[1,4,256,256]{3,2,1,0:T(8,128)}), f32[4,4,256,256]{3,2,1,0:T(8,128)}) %all-gather.12.cloned.1.call-update) | async-done | bytes 4194320 | tf_op jit(solution)/shard_map/all_gather | solution.py:21
  135.5 3.5 %multiply_add_fusion = f32[1,4,256,256]{3,2,1,0:T(8,128)} fusion(f32[4,4,256,256]{3,2,1,0:T(8,128)} %all-gather.12.cloned.1.call-done, f32[4]{0:T(128)S(1)} %bitcast_multiply_fusion.3, f32[4]{0:T(128)S(1)} %get-tuple-element.24, f32[4]{0:T(128)S(1)} %get-tuple-element.23, f32[4]{0:T(128)S(1)} %get-tuple-element.22), kind=kLoop, calls=%fused_computation.50 | loop fusion | flops 1835008 | bytes 5242944 | tf_op jit(solution)/shard_map/add | solution.py:34
  139.0 7.7 %all-gather.4 = f32[4,1,4]{2,1,0:T(1,128)S(1)} all-gather(f32[1,1,4]{2,1,0:T(1,128)S(1)} %get-tuple-element.21), channel_id=1, replica_groups=mesh['gx'=4,'gy'=4,'gz_0'=4,'gz_1'=2] {'gx'}, dimensions={0}, use_global_device_ids=true | all-gather | bytes 80 | tf_op jit(solution)/shard_map/all_gather | solution.py:21
  146.8 3.3 %multiply_convert_fusion.1 = bf16[4,512,512]{2,1,0:T(8,128)(2,1)S(1)} fusion(bf16[512,4,256]{0,2,1:T(8,128)(2,1)S(1)} %bitcast.190, f32[4,512]{1,0:T(4,128)S(1)} %bitcast.202, pred[512,512]{1,0:T(8,128)(4,1)S(1)} %iota_compare_fusion, bf16[64,4,8,256]{3,2,1,0:T(8,128)(2,1)} %bitcast.199), kind=kOutput, calls=%fused_computation.1 | convolution fusion | flops 543162368 | bytes 4464640 | tf_op jit(solution)/shard_map/thd,shd->hts/dot_general | solution.py:79
  150.2 0.8 fusion.8
  151.0 0.5 copy-done.2
  151.5 1.4 fusion.5
  152.9 2.3 %copy.50 = bf16[512,1024]{1,0:T(8,128)(2,1)} copy(bf16[512,1024]{0,1:T(8,128)(2,1)} %bitcast.197) | data formatting | bytes 2097152
  155.3 3.6 %fusion.45 = f32[4,512,256]{1,2,0:T(8,128)} fusion(bf16[512,4,256]{0,2,1:T(8,128)(2,1)S(1)} %bitcast.187, bf16[4,512,512]{2,1,0:T(8,128)(2,1)} %copy-done.2), kind=kOutput, calls=%fused_computation.97 | convolution fusion | flops 536870912 | bytes 5242880 | tf_op jit(solution)/shard_map/hts,thd->shd/dot_general | solution.py:91
  158.9 4.7 %fusion.6 = f32[4,512,256]{1,2,0:T(8,128)} fusion(bf16[512,4,256]{0,2,1:T(8,128)(2,1)S(1)} %bitcast.192, bf16[512,4,256]{0,2,1:T(8,128)(2,1)S(1)} %bitcast.188, f32[4,512]{1,0:T(4,128)S(1)} %bitcast.203, pred[512,512]{1,0:T(8,128)(4,1)S(1)} %iota_compare_fusion, bf16[64,4,8,256]{3,2,1,0:T(8,128)(2,1)} %bitcast.193), kind=kOutput, calls=%fused_computation.13 | convolution fusion | flops 1080033280 | bytes 5513216 | tf_op jit(solution)/shard_map/hts,thd->shd/dot_general | solution.py:99
  163.6 24.2 %all-gather.14.cloned.1.call-done = f32[4,4,256,256]{3,2,1,0:T(8,128)} async-done(((f32[1,4,256,256]{3,2,1,0:T(8,128)}), f32[4,4,256,256]{3,2,1,0:T(8,128)}) %all-gather.14.cloned.1.call-update) | async-done | bytes 4194320 | tf_op jit(solution)/shard_map/all_gather | solution.py:21
  187.8 6.4 %fusion.19 = bf16[4,256,256]{2,1,0:T(8,128)(2,1)S(1)} fusion(f32[4,4,256,256]{3,2,1,0:T(8,128)} %all-gather.14.cloned.1.call-done, f32[4,4,256,256]{3,2,1,0:T(8,128)} %all-gather.12.cloned.1.call-done, f32[4,4,256,256]{3,2,1,0:T(8,128)} %all-gather.10.cloned.1.call-done, f32[8,256,256]{2,1,0:T(8,128)} %all-gather.16.cloned.1.call-done, ...), kind=kLoop, calls=%fused_computation.26 | loop fusion | flops 11796480 | bytes 15204638 | tf_op jit(solution)/shard_map/convert_element_type | solution.py:68
  194.2 1.5 fusion.1
  195.7 2.4 %copy.52 = bf16[512,1024]{1,0:T(8,128)(2,1)} copy(bf16[512,1024]{0,1:T(8,128)(2,1)} %bitcast.198) | data formatting | bytes 2097152
  198.1 2.7 %fusion.3 = bf16[512,4,256]{0,2,1:T(8,128)(2,1)} fusion(f32[4,512,256]{1,2,0:T(8,128)S(1)} %copy-done.1, bf16[4,256,256]{2,1,0:T(8,128)(2,1)S(1)} %fusion.19, f32[512,4]{0,1:T(4,128)S(1)} %get-tuple-element.15, bf16[64,4,8,256]{3,2,1,0:T(8,128)(2,1)} %bitcast.200), kind=kOutput, calls=%fused_computation.8 | convolution fusion | flops 270008320 | bytes 4726784 | tf_op jit(solution)/shard_map/thj,hij->thi/dot_general | solution.py:96
  200.8 2.3 %copy.51 = bf16[512,1024]{1,0:T(8,128)(2,1)} copy(bf16[512,1024]{0,1:T(8,128)(2,1)} %bitcast.196) | data formatting | bytes 2097152
  (38 shorter events, 1.1 us)
Async XLA Ops:
  7.2 144.3 %copy-start = (bf16[1,4,256,256]{3,2,1,0:T(8,128)(2,1)S(1)}, bf16[1,4,256,256]{3,2,1,0:T(8,128)(2,1)}, u32[]{:S(2)}) copy-start(bf16[1,4,256,256]{3,2,1,0:T(8,128)(2,1)} %param.11) | copy-start | bytes 1572868
  7.2 24.3 %all-gather.16.cloned.1.call-start = ((), (), s32[]{:S(2)}) async-start(), calls=%async_computation.3 | async-start | bytes 3145728 | tf_op jit(solution)/shard_map/all_gather | solution.py:21
  12.9 1.6 copy-start.7
  12.9 6.4 %copy-start.6 = (u32[128]{0:T(128)S(1)}, u32[128]{0:T(128)}, u32[]{:S(2)}) copy-start(u32[128]{0:T(128)} %constant.43) | copy-start | bytes 1540
  14.4 69.1 %all-gather.10.cloned.1.call-start = ((), (), s32[]{:S(2)}) async-start(), calls=%async_computation | async-start | bytes 5242880 | tf_op jit(solution)/shard_map/all_gather | solution.py:21
  34.2 101.3 %all-gather.12.cloned.1.call-start = ((), (), s32[]{:S(2)}) async-start(), calls=%async_computation.1 | async-start | bytes 5242880 | tf_op jit(solution)/shard_map/all_gather | solution.py:21
  87.0 100.7 %all-gather.14.cloned.1.call-start = ((), (), s32[]{:S(2)}) async-start(), calls=%async_computation.2 | async-start | bytes 5242880 | tf_op jit(solution)/shard_map/all_gather | solution.py:21
  146.8 3.4 %copy-start.3 = (bf16[512,1024]{1,0:T(8,128)(2,1)S(1)}, bf16[512,1024]{1,0:T(8,128)(2,1)}, u32[]{:S(2)}) copy-start(bf16[512,1024]{1,0:T(8,128)(2,1)} %param.7) | copy-start | bytes 3145732
  150.2 1.3 copy-start.2
  187.8 6.4 %copy-start.4 = (bf16[512,1024]{1,0:T(8,128)(2,1)S(1)}, bf16[512,1024]{1,0:T(8,128)(2,1)}, u32[]{:S(2)}) copy-start(bf16[512,1024]{1,0:T(8,128)(2,1)} %param.7) | copy-start | bytes 3145732
  187.8 6.4 %copy-start.5 = (f32[4,512,256]{1,2,0:T(8,128)S(1)}, f32[4,512,256]{1,2,0:T(8,128)}, u32[]{:S(2)}) copy-start(f32[4,512,256]{1,2,0:T(8,128)} %fusion.6) | copy-start | bytes 6291460
  195.7 2.4 %copy-start.1 = (f32[4,512,256]{1,2,0:T(8,128)S(1)}, f32[4,512,256]{1,2,0:T(8,128)}, u32[]{:S(2)}) copy-start(f32[4,512,256]{1,2,0:T(8,128)} %fusion.45) | copy-start | bytes 6291460
Sparse Core Ops, SparseCore 0:
  14.5 16.8 all-gather.15
  34.3 49.1 all-gather.9
  87.1 48.3 all-gather.11
  139.2 48.5 all-gather.13
where the time goes:
time: 210 us
  waiting for transfers between devices  116 us (55%)
  blocking collectives  27.6 us (13%)
  matrix products  19.5 us (9%)
  other arithmetic  18.1 us (9%)
  between operations  15.2 us (7%)
  local copies, waits for them, and re-layouts  12.9 us (6%)
    all_gather x4, waiting for transfers between devices, carried_in(): pieces = jax.tree.map(lambda part: lax.all_gather(part, axis), subtotal)  116 us
    all_gather x2, blocking collectives, carried_in(): pieces = jax.tree.map(lambda part: lax.all_gather(part, axis), subtotal)  15.3 us
    unnamed x2, blocking collectives  12.3 us
    unnamed x27, local copies, waits for them, and re-layouts  10.4 us
    add x3, other arithmetic, combine_states(): later_part[0][:, None, None] * earlier_part[1] + later_part[1]  9.7 us
    convert_element_type x1, other arithmetic, body(): grad_in = later_grads[1].astype(jnp.bfloat16)  6.41 us
    dot_general x1, matrix products, body(): jnp.einsum('hts,thd->shd', probs, grad_heads, preferred_element_type=jnp....  4.73 us
  transfers between devices with their start and end apart: 4, of which 4 were waited for; matrix products, arithmetic and copies ran while one was open for 8% of the time, Pallas kernels for 0%

commit v1 on v0

v1 whole, which is shorter than its diff:
```python
import jax
import jax.numpy as jnp
from jax import lax
from jax.experimental import pallas as pl
from jax.experimental.pallas import tpu as pltpu
from jax.sharding import PartitionSpec as P

F32 = jnp.float32
BF16 = jnp.bfloat16
MESH = pl.DeviceIdType.MESH
AXES = ("gx", "gy", "gz")
HEADS = 4
DIM = 256
ROWS = 512
HALF = DIM // 2
CHUNKS = 2
SIDE = 4
CHIPS = SIDE**3
PEERS = sorted(
    (
        (dx, dy, dz)
        for dx in range(SIDE)
        for dy in range(SIDE)
        for dz in range(SIDE)
        if (dx, dy, dz) != (0, 0, 0)
    ),
    key=lambda o: -sum(min(d, SIDE - d) for d in o),
)


def dot(a, b, contract):
    return lax.dot_general(a, b, ((contract[:1], contract[1:]), ((), ())), preferred_element_type=F32)


def columns(h):
    return pl.ds(h * DIM, DIM)


def wait_bytes(ref, sem):
    pltpu.make_async_copy(ref, ref, sem).wait()


def cumulative_rows(ld):
    high = ld.astype(BF16)
    rest = ld - high.astype(F32)
    middle = rest.astype(BF16)
    low = (rest - middle.astype(F32)).astype(BF16)
    upto = lax.broadcasted_iota(jnp.int32, (ROWS, ROWS), 0) <= lax.broadcasted_iota(
        jnp.int32, (ROWS, ROWS), 1
    )
    ones = jnp.where(upto, 1.0, 0.0).astype(BF16)
    return (
        dot(high, ones, (1, 0)) + dot(middle, ones, (1, 0)) + dot(low, ones, (1, 0))
    )


def exchange_kernel(
    q_hbm, k_hbm, v_hbm, g_hbm, ld_hbm, st_hbm,
    qg, kp, vp, gi, te,
    q, k, v, g, ld, st,
    brow, bcol, start, local, other, total, arrived, carried, carry, pair_out, pair_in,
    own_decay, pair_decay, chip_decay, all_decay,
    in_sems, pair_sems, there_sems, back_sems, home_sems, decay_sems,
):
    gx, gy, gz = (lax.axis_index(a) for a in AXES)
    z, core = gz // 2, gz % 2
    me = (gx * SIDE + gy) * SIDE + z
    partner = (gx, gy, z * 2 + (1 - core))
    scale = DIM**-0.5

    def peer(o):
        x, y, w = (gx + o[0]) % SIDE, (gy + o[1]) % SIDE, (z + o[2]) % SIDE
        return (x, y, w * 2 + core), (x * SIDE + y) * SIDE + w, x // (SIDE // 2)

    loads = [
        pltpu.make_async_copy(a, b, in_sems.at[i])
        for i, (a, b) in enumerate(
            ((ld_hbm, ld), (q_hbm, q), (g_hbm, g), (k_hbm, k), (v_hbm, v), (st_hbm, st))
        )
    ]
    for copy in loads:
        copy.start()
    barrier = pltpu.get_barrier_semaphore()
    for o in PEERS:
        pl.semaphore_signal(barrier, inc=1, device_id=peer(o)[0], device_id_type=MESH)
    pl.semaphore_signal(barrier, inc=1, device_id=partner, device_id_type=MESH)

    loads[0].wait()
    b = cumulative_rows(jnp.concatenate([ld[...], jnp.zeros_like(ld)], axis=0))
    end = b[:, ROWS - 1 :]
    brow[...] = b
    bcol[...] = b.T
    start[...] = (scale * jnp.exp(b)).T
    te[...] = jnp.exp(end - b).T
    own_decay[...] = jnp.broadcast_to(jnp.exp(end), (8, 128))

    loads[1].wait()
    loads[2].wait()
    for h in range(HEADS):
        decayed = (q[:, columns(h)].astype(F32) * start[:, h : h + 1]).astype(BF16)
        gh = g[:, columns(h)]
        for half in range(2):
            local[h, half] = dot(decayed[:, half * HALF : (half + 1) * HALF], gh, (0, 0))

    pl.semaphore_wait(barrier, len(PEERS) + 1)

    swap_decay = pltpu.make_async_remote_copy(
        src_ref=own_decay, dst_ref=pair_decay, send_sem=decay_sems.at[0], recv_sem=decay_sems.at[1],
        device_id=partner, device_id_type=MESH,
    )
    swap_decay.start()
    swaps = []
    for ch in range(CHUNKS):
        for i in range(2):
            h = ch * 2 + i
            swaps.append(
                pltpu.make_async_remote_copy(
                    src_ref=local.at[h, 1 - core], dst_ref=other.at[h],
                    send_sem=pair_sems.at[0, h], recv_sem=pair_sems.at[1, h],
                    device_id=partner, device_id_type=MESH,
                )
            )
            swaps[-1].start()

    first = core == 0
    swap_decay.wait_recv()
    mine, theirs = own_decay[...], pair_decay[...]
    product = mine * theirs
    for i in range(2):
        chip_decay[i] = jnp.concatenate([product[i : i + 1], product[2 + i : 3 + i]], axis=0)
    all_decay[me] = chip_decay[gx // (SIDE // 2)]
    own_factor = jnp.where(first, 1.0, theirs)
    pair_factor = jnp.where(first, mine, 1.0)

    def send_all(source, target, by_sender, sems):
        for o in PEERS:
            device, theirs_at, _ = peer(o)
            pltpu.make_async_remote_copy(
                src_ref=source.at[theirs_at], dst_ref=target.at[me],
                send_sem=sems.at[0], recv_sem=sems.at[1],
                device_id=device, device_id_type=MESH,
            ).start()

    def wait_sent(ref, sems):
        wait_bytes(ref.at[pl.ds(0, CHIPS - 1)], sems.at[0])

    def wait_arrived(ref, sems):
        wait_bytes(ref.at[pl.ds(0, CHIPS - 1)], sems.at[1])

    for o in PEERS:
        device, _, half = peer(o)
        pltpu.make_async_remote_copy(
            src_ref=chip_decay.at[half], dst_ref=all_decay.at[me],
            send_sem=decay_sems.at[2], recv_sem=decay_sems.at[3],
            device_id=device, device_id_type=MESH,
        ).start()

    for ch in range(CHUNKS):
        for i in range(2):
            h = ch * 2 + i
            swaps[h].wait_recv()
            chip = local[h, core] * own_factor[h : h + 1, :1] + other[h] * pair_factor[h : h + 1, :1]
            for j in range(2):
                total[ch, pl.ds(i * 32 + j * 16, 16)] = chip[:, j * 128 : (j + 1) * 128].reshape(
                    16, 8, 128
                )
        send_all(total.at[ch], arrived.at[ch], None, there_sems.at[ch])
        arrived[ch, me] = total[ch, me]

    loads[3].wait()
    loads[4].wait()
    loads[5].wait()

    def inside(h):
        blocks = [[None, None], [None, None]]
        for s in range(2):
            for t in range(s, 2):
                at_s, at_t = pl.ds(s * 256, 256), pl.ds(t * 256, 256)
                gap = brow[h : h + 1, t * 256 : (t + 1) * 256] - bcol[at_s, h : h + 1]
                weight = jnp.exp(jnp.minimum(gap, 0.0)) * scale
                if s == t:
                    keep = lax.broadcasted_iota(jnp.int32, (256, 256), 0) <= lax.broadcasted_iota(
                        jnp.int32, (256, 256), 1
                    )
                    weight = jnp.where(keep, weight, 0.0)
                probs = (dot(k[at_s, columns(h)], q[at_t, columns(h)], (1, 1)) * weight).astype(BF16)
                grads = (dot(v[at_s, columns(h)], g[at_t, columns(h)], (1, 1)) * weight).astype(BF16)
                blocks[s][t] = (probs, grads)
        for s in range(2):
            at_s = pl.ds(s * 256, 256)
            kp[at_s, columns(h)] = sum(
                dot(blocks[s][t][1], q[pl.ds(t * 256, 256), columns(h)], (1, 0)) for t in range(s, 2)
            )
            vp[at_s, columns(h)] = sum(
                dot(blocks[s][t][0], g[pl.ds(t * 256, 256), columns(h)], (1, 0)) for t in range(s, 2)
            )
        for t in range(2):
            at_t = pl.ds(t * 256, 256)
            inner = sum(
                dot(blocks[s][t][1], k[pl.ds(s * 256, 256), columns(h)], (0, 0)) for s in range(t + 1)
            )
            from_state = dot(g[at_t, columns(h)], st[0, h], (1, 1)) * start[at_t, h : h + 1]
            qg[at_t, columns(h)] = (inner + from_state).astype(BF16)

    inside(0)
    inside(1)

    wait_arrived(all_decay, decay_sems.at[pl.ds(2, 2)])
    for ch in range(CHUNKS):
        wait_arrived(arrived.at[ch], there_sems.at[ch])
        running = jnp.zeros((8, 128), F32)
        for m in reversed(range(CHIPS)):
            carried[ch, m] = running
            running = running * all_decay[m, ch : ch + 1] + arrived[ch, m]
        send_all(carried.at[ch], carry.at[ch], None, back_sems.at[ch])
        carry[ch, me] = carried[ch, me]

    inside(2)
    inside(3)

    own_a, own_b = jnp.where(first, theirs, 1.0), jnp.where(first, 1.0, 0.0)
    out_a, out_b = jnp.where(first, 1.0, mine), jnp.where(first, 0.0, 1.0)
    homes = []
    for ch in range(CHUNKS):
        wait_arrived(carry.at[ch], back_sems.at[ch])
        for i in range(2):
            h = ch * 2 + i
            later = jnp.concatenate(
                [carry[ch, pl.ds(i * 32 + j * 16, 16)].reshape(128, 128) for j in range(2)], axis=1
            )
            pair_out[h] = later * out_a[h : h + 1, :1] + local[h, core] * out_b
            homes.append(
                pltpu.make_async_remote_copy(
                    src_ref=pair_out.at[h], dst_ref=pair_in.at[h],
                    send_sem=home_sems.at[0, h], recv_sem=home_sems.at[1, h],
                    device_id=partner, device_id_type=MESH,
                )
            )
            homes[-1].start()
            gi[h, core] = (later * own_a[h : h + 1, :1] + other[h] * own_b).astype(BF16)
    for h in range(HEADS):
        homes[h].wait_recv()
        gi[h, 1 - core] = pair_in[h].astype(BF16)

    swap_decay.wait_send()
    for copy in swaps + homes:
        copy.wait_send()
    wait_sent(all_decay, decay_sems.at[pl.ds(2, 2)])
    for ch in range(CHUNKS):
        wait_sent(total.at[ch], there_sems.at[ch])
        wait_sent(carried.at[ch], back_sems.at[ch])


def finish_kernel(k, v, qg_in, kp, vp, gi, te, qg, kg, vg):
    qg[...] = qg_in[...]
    h = pl.program_id(0)
    lane = lax.broadcasted_iota(jnp.int32, (ROWS, 8), 1)
    end = jnp.sum(jnp.where(lane == h, te[...], 0.0), axis=1, keepdims=True)
    grad_in = gi[0]
    kg[...] = (kp[...] + dot(v[...], grad_in, (1, 1)) * end).astype(BF16)
    vg[...] = (vp[...] + dot(k[...], grad_in, (1, 0)) * end).astype(BF16)


def body(queries, keys, values, out_grad, log_decay, saved_states):
    wide = (ROWS, HEADS * DIM)
    anywhere = pl.BlockSpec(memory_space=pltpu.HBM)
    vmem = pl.BlockSpec(memory_space=pltpu.VMEM)
    dma = pltpu.SemaphoreType.DMA
    pieces = pltpu.VMEM((CHUNKS, CHIPS, 8, 128), F32)
    halves = pltpu.VMEM((HEADS, HALF, DIM), F32)
    qg, kp, vp, gi, te = pl.pallas_call(
        exchange_kernel,
        out_shape=(
            jax.ShapeDtypeStruct(wide, BF16),
            jax.ShapeDtypeStruct(wide, F32),
            jax.ShapeDtypeStruct(wide, F32),
            jax.ShapeDtypeStruct((HEADS, 2, HALF, DIM), BF16),
            jax.ShapeDtypeStruct((ROWS, 8), F32),
        ),
        in_specs=[anywhere] * 6,
        out_specs=(vmem,) * 5,
        scratch_shapes=[
            pltpu.VMEM(wide, BF16), pltpu.VMEM(wide, BF16), pltpu.VMEM(wide, BF16), pltpu.VMEM(wide, BF16),
            pltpu.VMEM((HEADS, ROWS), F32), pltpu.VMEM((1, HEADS, DIM, DIM), BF16),
            pltpu.VMEM((8, ROWS), F32), pltpu.VMEM((ROWS, 8), F32), pltpu.VMEM((ROWS, 8), F32),
            pltpu.VMEM((HEADS, 2, HALF, DIM), F32), halves,
            pieces, pieces, pieces, pieces, halves, halves,
            pltpu.VMEM((8, 128), F32), pltpu.VMEM((8, 128), F32),
            pltpu.VMEM((2, CHUNKS, 128), F32), pltpu.VMEM((CHIPS, CHUNKS, 128), F32),
            dma((6,)), dma((2, HEADS)), dma((CHUNKS, 2)), dma((CHUNKS, 2)), dma((2, HEADS)), dma((4,)),
        ],
        compiler_params=pltpu.CompilerParams(
            collective_id=0, has_side_effects=True, vmem_limit_bytes=32 << 20
        ),
        cost_estimate=pl.CostEstimate(flops=4_000_000_000, bytes_accessed=8 << 20, transcendentals=0),
        name="exchange",
    )(queries, keys, values, out_grad, log_decay, saved_states)
    gi = gi.reshape(HEADS, DIM, DIM)
    by_head = pl.BlockSpec((ROWS, DIM), lambda h: (0, h))
    return pl.pallas_call(
        finish_kernel,
        grid=(HEADS,),
        out_shape=(jax.ShapeDtypeStruct(wide, BF16),) * 3,
        in_specs=[
            by_head, by_head, by_head, by_head, by_head,
            pl.BlockSpec((1, DIM, DIM), lambda h: (h, 0, 0)),
            pl.BlockSpec((ROWS, 8), lambda h: (0, 0)),
        ],
        out_specs=(by_head,) * 3,
        compiler_params=pltpu.CompilerParams(vmem_limit_bytes=16 << 20),
        cost_estimate=pl.CostEstimate(flops=600_000_000, bytes_accessed=8 << 20, transcendentals=0),
        name="finish",
    )(keys, values, qg, kp, vp, gi, te)


def solution(mesh):
    rows = P(AXES, None)
    return jax.shard_map(
        body,
        mesh=mesh,
        in_specs=(rows, rows, rows, rows, P(None, AXES), P(AXES, None, None, None)),
        out_specs=(rows, rows, rows),
        check_vma=False,
    )
```

time: 210 us -> 41.2 us (0.20)
  waiting for transfers between devices: 116 us -> 0 us
  Pallas kernels: 0 us -> 33.5 us
  blocking collectives: 27.6 us -> 0 us
  matrix products: 19.5 us -> 0 us
  other arithmetic: 18.1 us -> 0 us
  between operations: 15.2 us -> 0.65 us
  local copies, waits for them, and re-layouts: 12.9 us -> 6.63 us
    all_gather x4 -> x0, waiting for transfers between devices: 116 us -> none  [carried_in(): pieces = jax.tree.map(lambda part: lax.all_gather(part, axis), subtotal)]
    pallas_call x0 -> x2, Pallas kernels: none -> 33.5 us  [the longest x1 30.2 us: body(): pl.pallas_call(exchange_kernel, out_shape=(jax.ShapeDtypeStruct(wide, BF1...]
    dot_general x8 -> x0, matrix products: 19.5 us -> none  [the longest x1 4.73 us: body(): jnp.einsum('hts,thd->shd', probs, grad_heads, preferred_element_type=jnp....]
    all_gather x2 -> x0, blocking collectives: 15.3 us -> none  [carried_in(): pieces = jax.tree.map(lambda part: lax.all_gather(part, axis), subtotal)]
    unnamed x2 -> x0, blocking collectives: 12.3 us -> none
    add x3 -> x0, other arithmetic: 9.7 us -> none  [combine_states(): later_part[0][:, None, None] * earlier_part[1] + later_part[1]]
    convert_element_type x1 -> x0, other arithmetic: 6.41 us -> none  [body(): grad_in = later_grads[1].astype(jnp.bfloat16)]
    unnamed x27 -> x12, local copies, waits for them, and re-layouts: 10.4 us -> 6.63 us
  transfers between devices with their start and end apart: 4 -> 0, of which waited for: 4 -> 0; matrix products, arithmetic and copies ran while one was open for 8% -> 0% of each run, Pallas kernels for 0% -> 0%
where the time goes in v1:
time: 41.2 us; the launch traced here: 40.8 us
  Pallas kernels  33.5 us (81%)
  local copies, waits for them, and re-layouts  6.63 us (16%)
  between operations  0.65 us (2%)
    pallas_call x1, Pallas kernels, body(): pl.pallas_call(exchange_kernel, out_shape=(jax.ShapeDtypeStruct(wide, BF1...  30.2 us
    unnamed x12, local copies, waits for them, and re-layouts  6.63 us
    pallas_call x1, Pallas kernels, body(): pl.pallas_call(finish_kernel, grid=(HEADS,), out_shape=(jax.ShapeDtypeStr...  3.29 us

profile of v1, /device:TPU:1, one launch (start us, length us, event | category | flops | bytes accessed | tf_op | source)
XLA Modules:
  0.0 40.8 jit_solution(6245570699636165956)
XLA Ops:
  0.6 0.0 copy-start
  0.6 1.2 %copy-done = bf16[512,1024]{1,0:T(8,128)(2,1)S(1)} copy-done((bf16[512,1024]{1,0:T(8,128)(2,1)S(1)}, bf16[512,1024]{1,0:T(8,128)(2,1)}, u32[]{:S(2)}) %copy-start) | copy-done | bytes 1048600
  1.9 0.0 copy-start.1
  1.9 1.2 %copy-done.1 = bf16[512,1024]{1,0:T(8,128)(2,1)S(1)} copy-done((bf16[512,1024]{1,0:T(8,128)(2,1)S(1)}, bf16[512,1024]{1,0:T(8,128)(2,1)}, u32[]{:S(2)}) %copy-start.1) | copy-done | bytes 1048600
  3.1 0.0 copy-start.2
  3.1 1.2 %copy-done.2 = bf16[512,1024]{1,0:T(8,128)(2,1)S(1)} copy-done((bf16[512,1024]{1,0:T(8,128)(2,1)S(1)}, bf16[512,1024]{1,0:T(8,128)(2,1)}, u32[]{:S(2)}) %copy-start.2) | copy-done | bytes 1048600
  4.3 0.0 copy-start.3
  4.3 1.2 %copy-done.3 = bf16[512,1024]{1,0:T(8,128)(2,1)S(1)} copy-done((bf16[512,1024]{1,0:T(8,128)(2,1)S(1)}, bf16[512,1024]{1,0:T(8,128)(2,1)}, u32[]{:S(2)}) %copy-start.3) | copy-done | bytes 1048600
  5.5 0.0 copy-start.4
  5.5 1.0 %copy-done.4 = bf16[1,4,256,256]{3,2,1,0:T(8,128)(2,1)S(1)} copy-done((bf16[1,4,256,256]{3,2,1,0:T(8,128)(2,1)S(1)}, bf16[1,4,256,256]{3,2,1,0:T(8,128)(2,1)}, u32[]{:S(2)}) %copy-start.4) | copy-done | bytes 524312
  6.6 0.0 copy-start.5
  6.6 0.7 %copy-done.5 = f32[4,512]{1,0:T(4,128)S(1)} copy-done((f32[4,512]{1,0:T(4,128)S(1)}, f32[4,512]{1,0:T(4,128)}, u32[]{:S(2)}) %copy-start.5) | copy-done | bytes 8216
  7.3 30.2 %exchange.1 = (bf16[512,1024]{1,0:T(8,128)(2,1)S(1)}, f32[512,1024]{1,0:T(8,128)S(1)}, f32[512,1024]{1,0:T(8,128)S(1)}, bf16[4,2,128,256]{3,2,1,0:T(8,128)(2,1)S(1)}, f32[512,8]{1,0:T(8,128)S(1)}) custom-call(bf16[512,1024]{1,0:T(8,128)(2,1)S(1)} %copy-done.2, bf16[512,1024]{1,0:T(8,128)(2,1)S(1)} %copy-done, bf16[512,1024]{1,0:T(8,128)(2,1)S(1)} %copy-done.1, ...), custom_call_target="tpu_custom_call" | custom-call | flops 4000000000 | bytes 8388608 | tf_op jit(solution)/shard_map/exchange/pallas_call | solution.py:271
  37.5 3.3 %finish.1 = (bf16[512,1024]{1,0:T(8,128)(2,1)}, bf16[512,1024]{1,0:T(8,128)(2,1)}, bf16[512,1024]{1,0:T(8,128)(2,1)}) custom-call(bf16[512,1024]{1,0:T(8,128)(2,1)S(1)} %copy-done, bf16[512,1024]{1,0:T(8,128)(2,1)S(1)} %copy-done.1, bf16[512,1024]{1,0:T(8,128)(2,1)S(1)} %get-tuple-element.8.qg_in, f32[512,1024]{1,0:T(8,128)S(1)} %get-tuple-element.9.kp, ...), custom_call_target="tpu_custom_call" | custom-call | flops 600000000 | bytes 8388608 | tf_op jit(solution)/shard_map/finish/pallas_call | solution.py:300
Async XLA Ops:
  0.6 1.2 %copy-start = (bf16[512,1024]{1,0:T(8,128)(2,1)S(1)}, bf16[512,1024]{1,0:T(8,128)(2,1)}, u32[]{:S(2)}) copy-start(bf16[512,1024]{1,0:T(8,128)(2,1)} %k.1) | copy-start | bytes 3145732
  1.9 1.2 %copy-start.1 = (bf16[512,1024]{1,0:T(8,128)(2,1)S(1)}, bf16[512,1024]{1,0:T(8,128)(2,1)}, u32[]{:S(2)}) copy-start(bf16[512,1024]{1,0:T(8,128)(2,1)} %v.1) | copy-start | bytes 3145732
  3.1 1.2 %copy-start.2 = (bf16[512,1024]{1,0:T(8,128)(2,1)S(1)}, bf16[512,1024]{1,0:T(8,128)(2,1)}, u32[]{:S(2)}) copy-start(bf16[512,1024]{1,0:T(8,128)(2,1)} %q_hbm.1) | copy-start | bytes 3145732
  4.3 1.2 %copy-start.3 = (bf16[512,1024]{1,0:T(8,128)(2,1)S(1)}, bf16[512,1024]{1,0:T(8,128)(2,1)}, u32[]{:S(2)}) copy-start(bf16[512,1024]{1,0:T(8,128)(2,1)} %g_hbm.1) | copy-start | bytes 3145732
  5.5 1.0 %copy-start.4 = (bf16[1,4,256,256]{3,2,1,0:T(8,128)(2,1)S(1)}, bf16[1,4,256,256]{3,2,1,0:T(8,128)(2,1)}, u32[]{:S(2)}) copy-start(bf16[1,4,256,256]{3,2,1,0:T(8,128)(2,1)} %st_hbm.1) | copy-start | bytes 1572868
  6.6 0.7 %copy-start.5 = (f32[4,512]{1,0:T(4,128)S(1)}, f32[4,512]{1,0:T(4,128)}, u32[]{:S(2)}) copy-start(f32[4,512]{1,0:T(4,128)} %ld_hbm.1) | copy-start | bytes 24580

commit v2 on v1

--- a/solution.py
+++ b/solution.py
@@ -56,8 +56,8 @@
 
 def exchange_kernel(
     q_hbm, k_hbm, v_hbm, g_hbm, ld_hbm, st_hbm,
-    qg, kp, vp, gi, te,
-    q, k, v, g, ld, st,
+    qg, kg, vg,
+    q, k, v, g, ld, st, kp, vp, gi, te,
     brow, bcol, start, local, other, total, arrived, carried, carry, pair_out, pair_in,
     own_decay, pair_decay, chip_decay, all_decay,
     in_sems, pair_sems, there_sems, back_sems, home_sems, decay_sems,
@@ -241,6 +241,9 @@
     for h in range(HEADS):
         homes[h].wait_recv()
         gi[h, 1 - core] = pair_in[h].astype(BF16)
+        grad_in, to_end = gi[h].reshape(DIM, DIM), te[:, h : h + 1]
+        kg[:, columns(h)] = (kp[:, columns(h)] + dot(v[:, columns(h)], grad_in, (1, 1)) * to_end).astype(BF16)
+        vg[:, columns(h)] = (vp[:, columns(h)] + dot(k[:, columns(h)], grad_in, (1, 0)) * to_end).astype(BF16)
 
     swap_decay.wait_send()
     for copy in swaps + homes:
@@ -251,37 +254,35 @@
         wait_sent(carried.at[ch], back_sems.at[ch])
 
 
-def finish_kernel(k, v, qg_in, kp, vp, gi, te, qg, kg, vg):
-    qg[...] = qg_in[...]
-    h = pl.program_id(0)
-    lane = lax.broadcasted_iota(jnp.int32, (ROWS, 8), 1)
-    end = jnp.sum(jnp.where(lane == h, te[...], 0.0), axis=1, keepdims=True)
-    grad_in = gi[0]
-    kg[...] = (kp[...] + dot(v[...], grad_in, (1, 1)) * end).astype(BF16)
-    vg[...] = (vp[...] + dot(k[...], grad_in, (1, 0)) * end).astype(BF16)
-
-
-def body(queries, keys, values, out_grad, log_decay, saved_states):
-    wide = (ROWS, HEADS * DIM)
-    anywhere = pl.BlockSpec(memory_space=pltpu.HBM)
-    vmem = pl.BlockSpec(memory_space=pltpu.VMEM)
+def write_kernel(*refs):
+    count = len(refs) // 2
+    copies = [
+        pltpu.make_async_copy(source, target, refs[-1].at[i])
+        for i, (source, target) in enumerate(zip(refs[:count], refs[count:-1]))
+    ]
+    for copy in copies:
+        copy.start()
+    for copy in copies:
+        copy.wait()
+
+
+def body(*arrays):
+    wide = jax.ShapeDtypeStruct((ROWS, HEADS * DIM), BF16)
     dma = pltpu.SemaphoreType.DMA
+    hbm, vmem = (pl.BlockSpec(memory_space=space) for space in (pltpu.HBM, pltpu.VMEM))
+    rows = pltpu.VMEM(wide.shape, BF16)
+    sums = pltpu.VMEM(wide.shape, F32)
     pieces = pltpu.VMEM((CHUNKS, CHIPS, 8, 128), F32)
     halves = pltpu.VMEM((HEADS, HALF, DIM), F32)
-    qg, kp, vp, gi, te = pl.pallas_call(
+    grads = pl.pallas_call(
         exchange_kernel,
-        out_shape=(
-            jax.ShapeDtypeStruct(wide, BF16),
-            jax.ShapeDtypeStruct(wide, F32),
-            jax.ShapeDtypeStruct(wide, F32),
-            jax.ShapeDtypeStruct((HEADS, 2, HALF, DIM), BF16),
-            jax.ShapeDtypeStruct((ROWS, 8), F32),
-        ),
-        in_specs=[anywhere] * 6,
-        out_specs=(vmem,) * 5,
+        out_shape=(wide,) * 3,
+        in_specs=[hbm] * 6,
+        out_specs=(vmem,) * 3,
         scratch_shapes=[
-            pltpu.VMEM(wide, BF16), pltpu.VMEM(wide, BF16), pltpu.VMEM(wide, BF16), pltpu.VMEM(wide, BF16),
+            rows, rows, rows, rows,
             pltpu.VMEM((HEADS, ROWS), F32), pltpu.VMEM((1, HEADS, DIM, DIM), BF16),
+            sums, sums, pltpu.VMEM((HEADS, 2, HALF, DIM), BF16), pltpu.VMEM((ROWS, 8), F32),
             pltpu.VMEM((8, ROWS), F32), pltpu.VMEM((ROWS, 8), F32), pltpu.VMEM((ROWS, 8), F32),
             pltpu.VMEM((HEADS, 2, HALF, DIM), F32), halves,
             pieces, pieces, pieces, pieces, halves, halves,
@@ -290,27 +291,20 @@
             dma((6,)), dma((2, HEADS)), dma((CHUNKS, 2)), dma((CHUNKS, 2)), dma((2, HEADS)), dma((4,)),
         ],
         compiler_params=pltpu.CompilerParams(
-            collective_id=0, has_side_effects=True, vmem_limit_bytes=32 << 20
+            collective_id=0, has_side_effects=True, vmem_limit_bytes=40 << 20
         ),
         cost_estimate=pl.CostEstimate(flops=4_000_000_000, bytes_accessed=8 << 20, transcendentals=0),
         name="exchange",
-    )(queries, keys, values, out_grad, log_decay, saved_states)
-    gi = gi.reshape(HEADS, DIM, DIM)
-    by_head = pl.BlockSpec((ROWS, DIM), lambda h: (0, h))
+    )(*(pltpu.with_memory_space_constraint(x, pltpu.HBM) for x in arrays))
     return pl.pallas_call(
-        finish_kernel,
-        grid=(HEADS,),
-        out_shape=(jax.ShapeDtypeStruct(wide, BF16),) * 3,
-        in_specs=[
-            by_head, by_head, by_head, by_head, by_head,
-            pl.BlockSpec((1, DIM, DIM), lambda h: (h, 0, 0)),
-            pl.BlockSpec((ROWS, 8), lambda h: (0, 0)),
-        ],
-        out_specs=(by_head,) * 3,
-        compiler_params=pltpu.CompilerParams(vmem_limit_bytes=16 << 20),
-        cost_estimate=pl.CostEstimate(flops=600_000_000, bytes_accessed=8 << 20, transcendentals=0),
-        name="finish",
-    )(keys, values, qg, kp, vp, gi, te)
+        write_kernel,
+        out_shape=(wide,) * 3,
+        in_specs=[vmem] * 3,
+        out_specs=(hbm,) * 3,
+        scratch_shapes=[dma((3,))],
+        compiler_params=pltpu.CompilerParams(vmem_limit_bytes=8 << 20),
+        name="write",
+    )(*grads)
 
 
 def solution(mesh):

time: 41.2 us -> 33 us (0.80)
  local copies, waits for them, and re-layouts: 6.63 us -> 0 us
  Pallas kernels: 33.5 us -> 32.2 us
    unnamed x12 -> x0, local copies, waits for them, and re-layouts: 6.63 us -> none
    pallas_call x2, Pallas kernels: 33.5 us -> 32.2 us  [the longest x1 30.5 us: body(): pl.pallas_call(exchange_kernel, out_shape=(wide,) * 3, in_specs=[hbm] * 6...]
where the time goes in v2:
time: 33 us; the launch traced here: 32.9 us
  Pallas kernels  32.2 us (98%)
  between operations  0.64 us (2%)
    pallas_call x1, Pallas kernels, body(): pl.pallas_call(exchange_kernel, out_shape=(wide,) * 3, in_specs=[hbm] * 6...  30.5 us
    pallas_call x1, Pallas kernels, body(): pl.pallas_call(write_kernel, out_shape=(wide,) * 3, in_specs=[vmem] * 3,...  1.69 us

profile of v2, /device:TPU:1, one launch (start us, length us, event | category | flops | bytes accessed | tf_op | source)
XLA Modules:
  0.0 32.9 jit_solution(7286281102745979381)
XLA Ops:
  0.6 30.5 %exchange.1 = (bf16[512,1024]{1,0:T(8,128)(2,1)S(1)}, bf16[512,1024]{1,0:T(8,128)(2,1)S(1)}, bf16[512,1024]{1,0:T(8,128)(2,1)S(1)}) custom-call(bf16[512,1024]{1,0:T(8,128)(2,1)} %q_hbm.1, bf16[512,1024]{1,0:T(8,128)(2,1)} %k_hbm.1, bf16[512,1024]{1,0:T(8,128)(2,1)} %v_hbm.1, bf16[512,1024]{1,0:T(8,128)(2,1)} %g_hbm.1, f32[4,512]{1,0:T(4,128)} %ld_hbm.1, ...), custom_call_target="tpu_custom_call" | custom-call | flops 4000000000 | bytes 8388608 | tf_op jit(solution)/shard_map/exchange/pallas_call | solution.py:277
  31.2 1.7 %write.1 = (bf16[512,1024]{1,0:T(8,128)(2,1)}, bf16[512,1024]{1,0:T(8,128)(2,1)}, bf16[512,1024]{1,0:T(8,128)(2,1)}) custom-call(bf16[512,1024]{1,0:T(8,128)(2,1)S(1)} %get-tuple-element.6.refs_0_, bf16[512,1024]{1,0:T(8,128)(2,1)S(1)} %get-tuple-element.7.refs_1_, bf16[512,1024]{1,0:T(8,128)(2,1)S(1)} %get-tuple-element.8.refs_2_), custom_call_target="tpu_custom_call" | custom-call | tf_op jit(solution)/shard_map/write/pallas_call | solution.py:299
